TPU v7x, 128 devices: a whole 4x4x4 slice. The times are simulated.
128 devices in a mesh: gx: 8 (over x_lo, y), gy: 16 (over z, x_hi, core).
Axes of the slice: x: 4 (x_hi: 2, x_lo: 2; x = x_hi * 2 + x_lo), y: 4, z: 4, core: 2. Of those that a mesh axis runs over, the one named last changes fastest.
Arguments:
- expert_grad: bfloat16 [8, 512, 14336], P('gx', None, 'gy'), may hold values from -40000 to 40000
- attn_grad: bfloat16 [8, 2048, 4096], P('gx', None, 'gy'), may hold values from -40000 to 40000
- expert_master: float32 [4096, 14336], P(('gx', 'gy')), may hold values from -0.75 to 0.75
- expert_moment: float32 [4096, 14336], P(('gx', 'gy')), may hold values from -6 to 6
- expert_second: float32 [4096, 14336], P(('gx', 'gy')), may hold values from 0.1 to 4
- attn_master: float32 [2048, 4096], P(('gx', 'gy')), may hold values from -0.75 to 0.75
- attn_moment: float32 [2048, 4096], P(('gx', 'gy')), may hold values from -6 to 6
- attn_second: float32 [2048, 4096], P(('gx', 'gy')), may hold values from 0.1 to 4
Outputs:
- expert_master_new: float32 [4096, 14336], P(('gx', 'gy'))
- expert_moment_new: float32 [4096, 14336], P(('gx', 'gy'))
- expert_second_new: float32 [4096, 14336], P(('gx', 'gy'))
- attn_master_new: float32 [2048, 4096], P(('gx', 'gy'))
- attn_moment_new: float32 [2048, 4096], P(('gx', 'gy'))
- attn_second_new: float32 [2048, 4096], P(('gx', 'gy'))
- expert_weight: bfloat16 [8, 512, 14336], P('gx', None, 'gy')
- attn_weight: bfloat16 [2048, 4096], P(None, 'gy')
All inputs are finite; a program needn't handle non-finite values.
Results may differ from a plain program's by a relative error of at most 0.001.
Values may be sent and summed in bfloat16 or wider, within the bound.
No kernel may reach another device: no remote copies, remote signals or barrier semaphores. Data moves between devices by JAX's collectives and lax.ppermute only.
A program may use at most 64 MiB of HBM per device.

v0:
```python
import jax
import jax.numpy as jnp
from jax import lax
from jax.sharding import Mesh
from jax.sharding import PartitionSpec as P

NUMEL = 67108864
GY = ("gy_0", "gy_1", "gy_2")
GX = ("gx_0", "gx_1")
GX_GY = ("gx_0", "gx_1", "gy_0", "gy_1", "gy_2")
beta_one = 0.9
beta_two = 0.95
learn_rate = 0.01
weight_decay = 0.1
adam_eps = 1e-08
bias_one = 1.0 - 0.9**20
bias_two = 1.0 - 0.95**20


def cut_along(shard, dim, devices):
    before, after = (shard.shape[:dim], shard.shape[dim + 1 :])
    return jnp.moveaxis(shard.reshape(*before, devices, -1, *after), dim, 0)


def sum_at_owner(shard, axis, dim):
    parts = cut_along(shard, dim, lax.axis_size(axis))
    arrived = lax.all_to_all(parts, axis, split_axis=0, concat_axis=0, tiled=True)
    return arrived.sum(axis=0)


def one_axis_at_a_time(shard, axes):
    for axis in axes:
        shard = lax.psum(shard, axis)
    return shard


def joined_along(parts, dim):
    parts = jnp.moveaxis(parts, 0, dim)
    dims = parts.shape
    return parts.reshape(*dims[:dim], dims[dim] * dims[dim + 1], *dims[dim + 2 :])


def from_everyone(shard, axis):
    copies = jnp.broadcast_to(shard, (lax.axis_size(axis), *shard.shape))
    return lax.all_to_all(copies, axis, split_axis=0, concat_axis=0, tiled=True)


def gather_directly(shard, axis, dim):
    return joined_along(from_everyone(shard, axis), dim)


def adam_update(gradient, master, moment, second, clip_factor):
    scaled = clip_factor * gradient
    moment_new = beta_one * moment + (1.0 - beta_one) * scaled
    second_new = beta_two * second + (1.0 - beta_two) * scaled * scaled
    update = moment_new / bias_one / (jnp.sqrt(second_new / bias_two) + adam_eps)
    master_new = master - learn_rate * (update + weight_decay * master)
    return (master_new, moment_new, second_new)


def squares(expert_part, attn_part):
    wide = expert_part.astype(jnp.float32)
    return jnp.sum(wide * wide) + jnp.sum(attn_part * attn_part)


def regroup(flat_grad, owned):
    expert_group = lax.all_to_all(flat_grad, GY, split_axis=0, concat_axis=1, tiled=True)
    attn_group = lax.all_to_all(owned, GY, split_axis=0, concat_axis=1, tiled=True)
    return (expert_group, attn_group)


def local(
    expert_grad,
    attn_grad,
    expert_master,
    expert_moment,
    expert_second,
    attn_master,
    attn_moment,
    attn_second,
):
    local_experts, expert_rows, col_share = expert_grad.shape
    flat_grad = expert_grad.reshape(local_experts * expert_rows, col_share)
    attn_local = attn_grad.reshape(attn_grad.shape[1], attn_grad.shape[2]).astype(jnp.float32)
    owned = sum_at_owner(attn_local, GX, 0)
    expert_group, attn_group = regroup(flat_grad, owned)
    total = one_axis_at_a_time(squares(expert_group, attn_group), GX_GY)
    clip_factor = 1.0 / jnp.sqrt(total / NUMEL + 1e-06)
    e_master, e_moment, e_second = adam_update(
        expert_group.astype(jnp.float32), expert_master, expert_moment, expert_second, clip_factor
    )
    a_master, a_moment, a_second = adam_update(
        attn_group, attn_master, attn_moment, attn_second, clip_factor
    )
    expert_back, attn_back = (
        lax.all_to_all(e_master.astype(jnp.bfloat16), GY, split_axis=1, concat_axis=0, tiled=True),
        lax.all_to_all(a_master.astype(jnp.bfloat16), GY, split_axis=1, concat_axis=0, tiled=True),
    )
    expert_weight = expert_back.reshape(local_experts, expert_rows, col_share)
    attn_weight = gather_directly(attn_back, GX, 0)
    return (e_master, e_moment, e_second, a_master, a_moment, a_second, expert_weight, attn_weight)


def solution(mesh):
    split = Mesh(mesh.devices.reshape(2, 4, 4, 2, 2), ("gx_0", "gx_1", "gy_0", "gy_1", "gy_2"))
    placed = (
        P(GX, None, GY),
        P(GX, None, GY),
        P(GX_GY, None),
        P(GX_GY, None),
        P(GX_GY, None),
        P(GX_GY, None),
        P(GX_GY, None),
        P(GX_GY, None),
    )
    return jax.shard_map(
        local,
        mesh=split,
        in_specs=placed,
        out_specs=(
            P(GX_GY, None),
            P(GX_GY, None),
            P(GX_GY, None),
            P(GX_GY, None),
            P(GX_GY, None),
            P(GX_GY, None),
            P(GX, None, GY),
            P(None, GY),
        ),
        check_vma=False,
    )
```

profile of v0, /device:TPU:1, one launch (start us, length us, event | category | flops | bytes accessed | tf_op | source)
XLA Modules:
  0.0 165.8 jit_solution(18254513173904601893)
XLA Ops:
  0.6 1.4 convert.1
  2.0 31.5 %all_to_all.71 = f32[8,256,256]{2,1,0:T(8,128)S(1)} all-to-all(f32[8,256,256]{2,1,0:T(8,128)S(1)} %convert.1), channel_id=1, replica_groups=mesh['gx_0'=2,'gx_1'=4,'gy_0'=4,'gy_1'=2,'gy_2'=2] {'gx_0','gx_1'}, dimensions={0} | all-to-all | bytes 4194304 | tf_op jit(solution)/shard_map/all_to_all | solution.py:27
  33.5 9.9 %all-to-all-start = ((bf16[16,32,896]{2,1,0:T(8,128)(2,1)}), bf16[16,32,896]{2,1,0:T(8,128)(2,1)S(1)}, u32[]{:S(2)}, u32[]{:S(2)}) async-start(bf16[16,32,896]{2,1,0:T(8,128)(2,1)} %bitcast.34), calls=%async_computation | async-start | bytes 1835008 | tf_op jit(solution)/shard_map/all_to_all | solution.py:67
  43.4 0.8 reduce_sum.28
  44.3 14.8 %all-to-all-done = bf16[16,32,896]{2,1,0:T(8,128)(2,1)S(1)} async-done(((bf16[16,32,896]{2,1,0:T(8,128)(2,1)}), bf16[16,32,896]{2,1,0:T(8,128)(2,1)S(1)}, u32[]{:S(2)}, u32[]{:S(2)}) %all-to-all-start) | async-done | bytes 917536 | tf_op jit(solution)/shard_map/all_to_all | solution.py:67
  59.1 4.3 %all-to-all-start.2 = ((f32[16,16,256]{2,1,0:T(8,128)}), f32[16,16,256]{2,1,0:T(8,128)S(1)}, u32[]{:S(2)}, u32[]{:S(2)}) async-start(f32[16,16,256]{2,1,0:T(8,128)} %bitcast.2), calls=%async_computation.2 | async-start | bytes 524288 | tf_op jit(solution)/shard_map/all_to_all | solution.py:68
  63.4 1.1 fusion
  64.5 7.7 %all-to-all-done.2 = f32[16,16,256]{2,1,0:T(8,128)S(1)} async-done(((f32[16,16,256]{2,1,0:T(8,128)}), f32[16,16,256]{2,1,0:T(8,128)S(1)}, u32[]{:S(2)}, u32[]{:S(2)}) %all-to-all-start.2) | async-done | bytes 262176 | tf_op jit(solution)/shard_map/all_to_all | solution.py:68
  72.1 0.7 multiply_reduce_fusion
  74.1 4.3 %psum.35 = f32[]{:T(128)} all-reduce(f32[]{:T(128)S(6)} %add.46), channel_id=1, replica_groups=mesh['gx_0'=2,'gx_1'=4,'gy_0'=4,'gy_1'=2,'gy_2'=2] {'gx_0'}, use_global_device_ids=true, to_apply=%region_3.0 | all-reduce | flops 1 | bytes 8 | tf_op jit(solution)/shard_map/psum | solution.py:33
  78.4 7.1 %psum.36 = f32[]{:T(128)} all-reduce(f32[]{:T(128)} %psum.35), channel_id=1, replica_groups=mesh['gx_0'=2,'gx_1'=4,'gy_0'=4,'gy_1'=2,'gy_2'=2] {'gx_1'}, use_global_device_ids=true, to_apply=%region_4.0 | all-reduce | flops 1 | bytes 8 | tf_op jit(solution)/shard_map/psum | solution.py:33
  85.5 7.5 %psum.37 = f32[]{:T(128)} all-reduce(f32[]{:T(128)} %psum.36), channel_id=1, replica_groups=mesh['gx_0'=2,'gx_1'=4,'gy_0'=4,'gy_1'=2,'gy_2'=2] {'gy_0'}, use_global_device_ids=true, to_apply=%region_5.0 | all-reduce | flops 1 | bytes 8 | tf_op jit(solution)/shard_map/psum | solution.py:33
  93.0 5.9 %psum.38 = f32[]{:T(128)} all-reduce(f32[]{:T(128)} %psum.37), channel_id=1, replica_groups=mesh['gx_0'=2,'gx_1'=4,'gy_0'=4,'gy_1'=2,'gy_2'=2] {'gy_1'}, use_global_device_ids=true, to_apply=%region_6.0 | all-reduce | flops 1 | bytes 8 | tf_op jit(solution)/shard_map/psum | solution.py:33
  98.9 9.7 %psum.39 = f32[]{:T(128)} all-reduce(f32[]{:T(128)} %psum.38), channel_id=1, replica_groups=mesh['gx_0'=2,'gx_1'=4,'gy_0'=4,'gy_1'=2,'gy_2'=2] {'gy_2'}, use_global_device_ids=true, to_apply=%region_7.0 | all-reduce | flops 1 | bytes 8 | tf_op jit(solution)/shard_map/psum | solution.py:33
  109.3 0.2 fusion.1
  109.5 0.0 copy-start
  109.5 0.0 copy-start.1
  109.5 0.0 copy-start.2
  109.5 0.1 copy.37
  109.7 0.7 copy-done
  110.5 0.1 copy-done.1
  110.5 0.1 copy-done.2
  110.6 1.0 fusion.4
  111.6 0.7 copy.42
  112.3 3.6 %all-to-all-start.4 = ((bf16[16,16,256]{2,0,1:T(8,128)(2,1)}), bf16[16,16,256]{2,0,1:T(8,128)(2,1)S(1)}, u32[]{:S(2)}, u32[]{:S(2)}) async-start(bf16[16,16,256]{2,0,1:T(8,128)(2,1)} %bitcast.26), calls=%async_computation.4 | async-start | bytes 262144 | tf_op jit(solution)/shard_map/all_to_all | solution.py:97
  115.9 5.9 %fusion.6 = (bf16[32,14336]{1,0:T(8,128)(2,1)S(1)}, f32[32,14336]{1,0:T(8,128)}, f32[32,14336]{1,0:T(8,128)}, f32[32,14336]{1,0:T(8,128)}) fusion(f32[32,14336]{1,0:T(8,128)} %param.10, f32[32,14336]{1,0:T(8,128)S(1)} %bitcast.27, f32[32,14336]{1,0:T(8,128)} %param.11, f32[32,14336]{1,0:T(8,128)} %param.12), kind=kLoop, calls=%fused_computation.17 | loop fusion | flops 7340032 | bytes 13762560 | tf_op jit(solution)/shard_map/convert_element_type | solution.py:96
  121.9 0.1 copy.41
  121.9 1.7 %all-to-all-done.4 = bf16[16,16,256]{2,0,1:T(8,128)(2,1)S(1)} async-done(((bf16[16,16,256]{2,0,1:T(8,128)(2,1)}), bf16[16,16,256]{2,0,1:T(8,128)(2,1)S(1)}, u32[]{:S(2)}, u32[]{:S(2)}) %all-to-all-start.4) | async-done | bytes 131104 | tf_op jit(solution)/shard_map/all_to_all | solution.py:97
  123.6 20.8 %all_to_all.72 = bf16[32,16,896]{2,0,1:T(8,128)(2,1)S(1)} all-to-all(bf16[32,16,896]{2,0,1:T(8,128)(2,1)S(1)} %bitcast.30), channel_id=1, replica_groups=mesh['gx_0'=2,'gx_1'=4,'gy_0'=4,'gy_1'=2,'gy_2'=2] {'gy_0','gy_1','gy_2'}, dimensions={1} | all-to-all | bytes 1835008 | tf_op jit(solution)/shard_map/all_to_all | solution.py:96
  144.4 1.0 broadcast_in_dim.3
  145.4 3.6 %all-to-all-start.5 = ((bf16[8,256,256]{2,1,0:T(8,128)(2,1)}), bf16[8,256,256]{2,1,0:T(8,128)(2,1)S(1)}, u32[]{:S(2)}, u32[]{:S(2)}) async-start(bf16[8,256,256]{2,1,0:T(8,128)(2,1)} %broadcast_in_dim.3), calls=%async_computation.5 | async-start | bytes 2097152 | tf_op jit(solution)/shard_map/all_to_all | solution.py:45
  149.0 14.9 %all-to-all-done.5 = bf16[8,256,256]{2,1,0:T(8,128)(2,1)S(1)} async-done(((bf16[8,256,256]{2,1,0:T(8,128)(2,1)}), bf16[8,256,256]{2,1,0:T(8,128)(2,1)S(1)}, u32[]{:S(2)}, u32[]{:S(2)}) %all-to-all-start.5) | async-done | bytes 1048608 | tf_op jit(solution)/shard_map/all_to_all | solution.py:45
  163.9 0.9 copy.45
  164.8 1.0 copy.46
  (2 shorter events, 0.0 us)
Async XLA Ops:
  33.5 25.6 %all-to-all-start = ((bf16[16,32,896]{2,1,0:T(8,128)(2,1)}), bf16[16,32,896]{2,1,0:T(8,128)(2,1)S(1)}, u32[]{:S(2)}, u32[]{:S(2)}) async-start(bf16[16,32,896]{2,1,0:T(8,128)(2,1)} %bitcast.34), calls=%async_computation | async-start | bytes 1835008 | tf_op jit(solution)/shard_map/all_to_all | solution.py:67
  59.1 13.1 %all-to-all-start.2 = ((f32[16,16,256]{2,1,0:T(8,128)}), f32[16,16,256]{2,1,0:T(8,128)S(1)}, u32[]{:S(2)}, u32[]{:S(2)}) async-start(f32[16,16,256]{2,1,0:T(8,128)} %bitcast.2), calls=%async_computation.2 | async-start | bytes 524288 | tf_op jit(solution)/shard_map/all_to_all | solution.py:68
  109.5 1.0 copy-start
  109.5 1.0 copy-start.1
  109.5 1.1 copy-start.2
  112.3 11.3 %all-to-all-start.4 = ((bf16[16,16,256]{2,0,1:T(8,128)(2,1)}), bf16[16,16,256]{2,0,1:T(8,128)(2,1)S(1)}, u32[]{:S(2)}, u32[]{:S(2)}) async-start(bf16[16,16,256]{2,0,1:T(8,128)(2,1)} %bitcast.26), calls=%async_computation.4 | async-start | bytes 262144 | tf_op jit(solution)/shard_map/all_to_all | solution.py:97
  145.4 18.4 %all-to-all-start.5 = ((bf16[8,256,256]{2,1,0:T(8,128)(2,1)}), bf16[8,256,256]{2,1,0:T(8,128)(2,1)S(1)}, u32[]{:S(2)}, u32[]{:S(2)}) async-start(bf16[8,256,256]{2,1,0:T(8,128)(2,1)} %broadcast_in_dim.3), calls=%async_computation.5 | async-start | bytes 2097152 | tf_op jit(solution)/shard_map/all_to_all | solution.py:45
where the time goes:
time: 166 us
  blocking collectives  86.7 us (52%)
  waiting for transfers between devices  39.1 us (24%)
  starting transfers between devices  21.4 us (13%)
  other arithmetic  11.2 us (7%)
  local copies, waits for them, and re-layouts  4.71 us (3%)
  between operations  2.71 us (2%)
    psum x5, blocking collectives, one_axis_at_a_time(): shard = lax.psum(shard, axis)  34.5 us
    all_to_all x1, blocking collectives, sum_at_owner(): lax.all_to_all(parts, axis, split_axis=0, concat_axis=0, tiled=True)  31.5 us
    all_to_all x1, blocking collectives, local(): lax.all_to_all(e_master.astype(jnp.bfloat16), GY, split_axis=1, concat_ax...  20.8 us
    all_to_all x1, waiting for transfers between devices, from_everyone(): return lax.all_to_all(copies, axis, split_axis=0, concat_axis=0, tiled=True)  14.9 us
    all_to_all x1, waiting for transfers between devices, regroup(): lax.all_to_all(flat_grad, GY, split_axis=0, concat_axis=1, tiled=True)  14.8 us
    all_to_all x1, starting transfers between devices, regroup(): lax.all_to_all(flat_grad, GY, split_axis=0, concat_axis=1, tiled=True)  9.89 us
    all_to_all x1, waiting for transfers between devices, regroup(): lax.all_to_all(owned, GY, split_axis=0, concat_axis=1, tiled=True)  7.69 us
    convert_element_type x1, other arithmetic, local(): e_master.astype(jnp.bfloat16)  5.93 us
  transfers between devices with their start and end apart: 4, of which 4 were waited for; matrix products, arithmetic and copies ran while one was open for 5% of the time, Pallas kernels for 0%

commit v1 on v0

--- a/solution.py
+++ b/solution.py
@@ -17,6 +17,10 @@
 bias_two = 1.0 - 0.95**20
 
 
+def group_target(x_in, group_axis):
+    return lax.all_gather(x_in, group_axis).sum(axis=0)
+
+
 def cut_along(shard, dim, devices):
     before, after = (shard.shape[:dim], shard.shape[dim + 1 :])
     return jnp.moveaxis(shard.reshape(*before, devices, -1, *after), dim, 0)
@@ -30,7 +34,7 @@
 
 def one_axis_at_a_time(shard, axes):
     for axis in axes:
-        shard = lax.psum(shard, axis)
+        shard = group_target(shard, axis)
     return shard
 
 

time: 166 us -> 175 us (1.054)
  local copies, waits for them, and re-layouts: 4.71 us -> 14 us
  other arithmetic: 11.2 us -> 14.2 us
  blocking collectives: 86.7 us -> 83.7 us
    psum x5 -> x0, blocking collectives: 34.5 us -> none  [one_axis_at_a_time(): shard = lax.psum(shard, axis)]
    unnamed x0 -> x5, blocking collectives: none -> 31.4 us
    unnamed x8 -> x33, local copies, waits for them, and re-layouts: 2.8 us -> 12.1 us
    reduce_sum x0 -> x5, other arithmetic: none -> 3.02 us  [group_target(): return lax.all_gather(x_in, group_axis).sum(axis=0)]
where the time goes in v1:
time: 175 us; the launch traced here: 174 us
  blocking collectives  83.7 us (48%)
  waiting for transfers between devices  38.4 us (22%)
  starting transfers between devices  21.4 us (12%)
  other arithmetic  14.2 us (8%)
  local copies, waits for them, and re-layouts  14 us (8%)
  between operations  2.77 us (2%)
    all_to_all x1, blocking collectives, sum_at_owner(): lax.all_to_all(parts, axis, split_axis=0, concat_axis=0, tiled=True)  31.5 us
    unnamed x5, blocking collectives  31.4 us
    all_to_all x1, blocking collectives, local(): lax.all_to_all(e_master.astype(jnp.bfloat16), GY, split_axis=1, concat_ax...  20.8 us
    all_to_all x1, waiting for transfers between devices, from_everyone(): return lax.all_to_all(copies, axis, split_axis=0, concat_axis=0, tiled=True)  14.9 us
    all_to_all x1, waiting for transfers between devices, regroup(): lax.all_to_all(flat_grad, GY, split_axis=0, concat_axis=1, tiled=True)  14.8 us
    unnamed x33, local copies, waits for them, and re-layouts  12.1 us
    all_to_all x1, starting transfers between devices, regroup(): lax.all_to_all(flat_grad, GY, split_axis=0, concat_axis=1, tiled=True)  9.89 us
    all_to_all x1, waiting for transfers between devices, regroup(): lax.all_to_all(owned, GY, split_axis=0, concat_axis=1, tiled=True)  7.1 us
  transfers between devices with their start and end apart: 4, of which 4 were waited for; matrix products, arithmetic and copies ran while one was open for 5% of the time, Pallas kernels for 0%

profile of v1, /device:TPU:1, one launch (start us, length us, event | category | flops | bytes accessed | tf_op | source)
XLA Modules:
  0.0 174.5 jit_solution(13589009205403431990)
XLA Ops:
  0.6 1.4 convert.1
  2.0 31.5 %all_to_all.71 = f32[8,256,256]{2,1,0:T(8,128)S(1)} all-to-all(f32[8,256,256]{2,1,0:T(8,128)S(1)} %convert.1), channel_id=1, replica_groups=mesh['gx_0'=2,'gx_1'=4,'gy_0'=4,'gy_1'=2,'gy_2'=2] {'gx_0','gx_1'}, dimensions={0} | all-to-all | bytes 4194304 | tf_op jit(solution)/shard_map/all_to_all | solution.py:31
  33.5 9.9 %all-to-all-start = ((bf16[16,32,896]{2,1,0:T(8,128)(2,1)}), bf16[16,32,896]{2,1,0:T(8,128)(2,1)S(1)}, u32[]{:S(2)}, u32[]{:S(2)}) async-start(bf16[16,32,896]{2,1,0:T(8,128)(2,1)} %bitcast.44), calls=%async_computation | async-start | bytes 1835008 | tf_op jit(solution)/shard_map/all_to_all | solution.py:71
  43.4 0.0 copy-start.7
  43.4 0.0 copy-start.6
  43.4 0.0 copy-start.5
  43.5 0.0 copy-start.4
  43.5 0.0 copy-start.3
  43.5 0.8 reduce_sum.73
  44.3 14.8 %all-to-all-done = bf16[16,32,896]{2,1,0:T(8,128)(2,1)S(1)} async-done(((bf16[16,32,896]{2,1,0:T(8,128)(2,1)}), bf16[16,32,896]{2,1,0:T(8,128)(2,1)S(1)}, u32[]{:S(2)}, u32[]{:S(2)}) %all-to-all-start) | async-done | bytes 917536 | tf_op jit(solution)/shard_map/all_to_all | solution.py:71
  59.1 4.3 %all-to-all-start.2 = ((f32[16,16,256]{2,1,0:T(8,128)}), f32[16,16,256]{2,1,0:T(8,128)S(1)}, u32[]{:S(2)}, u32[]{:S(2)}) async-start(f32[16,16,256]{2,1,0:T(8,128)} %bitcast.2), calls=%async_computation.2 | async-start | bytes 524288 | tf_op jit(solution)/shard_map/all_to_all | solution.py:72
  63.4 0.0 copy-done.7
  63.4 0.6 dynamic-slice
  64.0 1.1 fusion
  65.0 7.1 %all-to-all-done.2 = f32[16,16,256]{2,1,0:T(8,128)S(1)} async-done(((f32[16,16,256]{2,1,0:T(8,128)}), f32[16,16,256]{2,1,0:T(8,128)S(1)}, u32[]{:S(2)}, u32[]{:S(2)}) %all-to-all-start.2) | async-done | bytes 262176 | tf_op jit(solution)/shard_map/all_to_all | solution.py:72
  72.1 0.7 multiply_reduce_fusion
  74.1 0.8 dynamic-update-slice
  74.9 0.0 copy-done.6
  74.9 0.6 dynamic-slice.1
  75.5 3.8 %all-reduce = f32[2]{0:T(128)S(1)} all-reduce(f32[2]{0:T(128)S(1)} %dynamic-update-slice), channel_id=1, replica_groups=mesh['gx_0'=2,'gx_1'=4,'gy_0'=4,'gy_1'=2,'gy_2'=2] {'gx_0'}, use_global_device_ids=true, to_apply=%add | all-reduce | flops 2 | bytes 16
  79.2 0.6 reduce_sum.75
  79.8 1.4 dynamic-update-slice.1
  81.2 0.0 copy-done.5
  81.2 0.6 dynamic-slice.2
  81.8 6.5 %all-reduce.1 = f32[4]{0:T(128)S(1)} all-reduce(f32[4]{0:T(128)S(1)} %dynamic-update-slice.1), channel_id=1, replica_groups=mesh['gx_0'=2,'gx_1'=4,'gy_0'=4,'gy_1'=2,'gy_2'=2] {'gx_1'}, use_global_device_ids=true, to_apply=%add.1 | all-reduce | flops 4 | bytes 32
  88.3 0.6 reduce_sum.76
  88.9 1.4 dynamic-update-slice.2
  90.3 0.0 copy-done.4
  90.3 0.6 dynamic-slice.3
  90.9 6.8 %all-reduce.2 = f32[4]{0:T(128)S(1)} all-reduce(f32[4]{0:T(128)S(1)} %dynamic-update-slice.2), channel_id=1, replica_groups=mesh['gx_0'=2,'gx_1'=4,'gy_0'=4,'gy_1'=2,'gy_2'=2] {'gy_0'}, use_global_device_ids=true, to_apply=%add.2 | all-reduce | flops 4 | bytes 32
  97.7 0.6 reduce_sum.77
  98.3 1.4 dynamic-update-slice.3
  99.7 0.0 copy-done.3
  99.7 0.6 dynamic-slice.4
  100.3 5.3 %all-reduce.3 = f32[2]{0:T(128)S(1)} all-reduce(f32[2]{0:T(128)S(1)} %dynamic-update-slice.3), channel_id=1, replica_groups=mesh['gx_0'=2,'gx_1'=4,'gy_0'=4,'gy_1'=2,'gy_2'=2] {'gy_1'}, use_global_device_ids=true, to_apply=%add.3 | all-reduce | flops 2 | bytes 16
  105.6 0.6 reduce_sum.78
  106.2 1.4 dynamic-update-slice.4
  107.6 9.1 %all-reduce.4 = f32[2]{0:T(128)S(1)} all-reduce(f32[2]{0:T(128)S(1)} %dynamic-update-slice.4), channel_id=1, replica_groups=mesh['gx_0'=2,'gx_1'=4,'gy_0'=4,'gy_1'=2,'gy_2'=2] {'gy_2'}, use_global_device_ids=true, to_apply=%add.4 | all-reduce | flops 2 | bytes 16
  116.7 0.6 reduce_sum.79
  118.0 0.2 fusion.1
  118.2 0.0 copy-start
  118.2 0.0 copy-start.1
  118.2 0.0 copy-start.2
  118.2 0.1 copy.37
  118.4 0.7 copy-done
  119.1 0.1 copy-done.1
  119.2 0.1 copy-done.2
  119.3 1.0 fusion.4
  120.3 0.7 copy.42
  121.0 3.6 %all-to-all-start.4 = ((bf16[16,16,256]{2,0,1:T(8,128)(2,1)}), bf16[16,16,256]{2,0,1:T(8,128)(2,1)S(1)}, u32[]{:S(2)}, u32[]{:S(2)}) async-start(bf16[16,16,256]{2,0,1:T(8,128)(2,1)} %bitcast.36), calls=%async_computation.4 | async-start | bytes 262144 | tf_op jit(solution)/shard_map/all_to_all | solution.py:101
  124.6 5.9 %fusion.6 = (bf16[32,14336]{1,0:T(8,128)(2,1)S(1)}, f32[32,14336]{1,0:T(8,128)}, f32[32,14336]{1,0:T(8,128)}, f32[32,14336]{1,0:T(8,128)}) fusion(f32[32,14336]{1,0:T(8,128)} %param.10, f32[32,14336]{1,0:T(8,128)S(1)} %bitcast.37, f32[32,14336]{1,0:T(8,128)} %param.11, f32[32,14336]{1,0:T(8,128)} %param.12), kind=kLoop, calls=%fused_computation.17 | loop fusion | flops 7340032 | bytes 13762560 | tf_op jit(solution)/shard_map/convert_element_type | solution.py:100
  130.5 0.1 copy.41
  130.6 1.7 all-to-all-done.4
  132.3 20.8 %all_to_all.72 = bf16[32,16,896]{2,0,1:T(8,128)(2,1)S(1)} all-to-all(bf16[32,16,896]{2,0,1:T(8,128)(2,1)S(1)} %bitcast.40), channel_id=1, replica_groups=mesh['gx_0'=2,'gx_1'=4,'gy_0'=4,'gy_1'=2,'gy_2'=2] {'gy_0','gy_1','gy_2'}, dimensions={1} | all-to-all | bytes 1835008 | tf_op jit(solution)/shard_map/all_to_all | solution.py:100
  153.1 1.0 broadcast_in_dim.3
  154.1 3.6 %all-to-all-start.5 = ((bf16[8,256,256]{2,1,0:T(8,128)(2,1)}), bf16[8,256,256]{2,1,0:T(8,128)(2,1)S(1)}, u32[]{:S(2)}, u32[]{:S(2)}) async-start(bf16[8,256,256]{2,1,0:T(8,128)(2,1)} %broadcast_in_dim.3), calls=%async_computation.5 | async-start | bytes 2097152 | tf_op jit(solution)/shard_map/all_to_all | solution.py:49
  157.7 14.9 %all-to-all-done.5 = bf16[8,256,256]{2,1,0:T(8,128)(2,1)S(1)} async-done(((bf16[8,256,256]{2,1,0:T(8,128)(2,1)}), bf16[8,256,256]{2,1,0:T(8,128)(2,1)S(1)}, u32[]{:S(2)}, u32[]{:S(2)}) %all-to-all-start.5) | async-done | bytes 1048608 | tf_op jit(solution)/shard_map/all_to_all | solution.py:49
  172.6 0.9 copy.56
  173.5 1.0 copy.57
  (7 shorter events, 0.0 us)
Async XLA Ops:
  33.5 25.6 %all-to-all-start = ((bf16[16,32,896]{2,1,0:T(8,128)(2,1)}), bf16[16,32,896]{2,1,0:T(8,128)(2,1)S(1)}, u32[]{:S(2)}, u32[]{:S(2)}) async-start(bf16[16,32,896]{2,1,0:T(8,128)(2,1)} %bitcast.44), calls=%async_computation | async-start | bytes 1835008 | tf_op jit(solution)/shard_map/all_to_all | solution.py:71
  43.4 20.0 %copy-start.7 = (u32[128]{0:T(128)S(1)}, u32[128]{0:T(128)}, u32[]{:S(2)}) copy-start(u32[128]{0:T(128)} %constant.46) | copy-start | bytes 1540
  43.4 31.5 %copy-start.6 = (u32[128]{0:T(128)S(1)}, u32[128]{0:T(128)}, u32[]{:S(2)}) copy-start(u32[128]{0:T(128)} %constant.51) | copy-start | bytes 1540
  43.4 37.8 %copy-start.5 = (u32[128]{0:T(128)S(1)}, u32[128]{0:T(128)}, u32[]{:S(2)}) copy-start(u32[128]{0:T(128)} %constant.56) | copy-start | bytes 1540
  43.5 46.9 %copy-start.4 = (u32[128]{0:T(128)S(1)}, u32[128]{0:T(128)}, u32[]{:S(2)}) copy-start(u32[128]{0:T(128)} %constant.61) | copy-start | bytes 1540
  43.5 56.3 %copy-start.3 = (u32[128]{0:T(128)S(1)}, u32[128]{0:T(128)}, u32[]{:S(2)}) copy-start(u32[128]{0:T(128)} %constant.66) | copy-start | bytes 1540
  59.1 13.1 %all-to-all-start.2 = ((f32[16,16,256]{2,1,0:T(8,128)}), f32[16,16,256]{2,1,0:T(8,128)S(1)}, u32[]{:S(2)}, u32[]{:S(2)}) async-start(f32[16,16,256]{2,1,0:T(8,128)} %bitcast.2), calls=%async_computation.2 | async-start | bytes 524288 | tf_op jit(solution)/shard_map/all_to_all | solution.py:72
  118.2 1.0 copy-start
  118.2 1.0 copy-start.1
  118.2 1.1 copy-start.2
  121.0 11.3 %all-to-all-start.4 = ((bf16[16,16,256]{2,0,1:T(8,128)(2,1)}), bf16[16,16,256]{2,0,1:T(8,128)(2,1)S(1)}, u32[]{:S(2)}, u32[]{:S(2)}) async-start(bf16[16,16,256]{2,0,1:T(8,128)(2,1)} %bitcast.36), calls=%async_computation.4 | async-start | bytes 262144 | tf_op jit(solution)/shard_map/all_to_all | solution.py:101
  154.1 18.4 %all-to-all-start.5 = ((bf16[8,256,256]{2,1,0:T(8,128)(2,1)}), bf16[8,256,256]{2,1,0:T(8,128)(2,1)S(1)}, u32[]{:S(2)}, u32[]{:S(2)}) async-start(bf16[8,256,256]{2,1,0:T(8,128)(2,1)} %broadcast_in_dim.3), calls=%async_computation.5 | async-start | bytes 2097152 | tf_op jit(solution)/shard_map/all_to_all | solution.py:49
